TPU v7x, 32 devices: a whole 2x2x4 slice. The times are simulated.
32 devices in a mesh: freq: 4 (over y, x), space: 8 (over z, core).
Axes of the slice: x: 2, y: 2, z: 4, core: 2. Of those that a mesh axis runs over, the one named last changes fastest.
Arguments:
- spectra: bfloat16 [2, 256, 24, 32768], P(None, 'freq', None, 'space'), may hold values from -6 to 6
- eigvecs: bfloat16 [2, 256, 4, 32768], P(None, 'freq', None, 'space'), may hold values from -6 to 6
- weights: bfloat16 [32768], P('space'), may hold values from 0.19921875 to 5
Outputs:
- filtered: float32 [3200, 32768], P(None, ('space', 'freq'))
All inputs are finite; a program needn't handle non-finite values.
Results may differ from a plain program's by a relative error of at most 0.004.
Values may be sent and summed in bfloat16 or wider, within the bound.
A program may use at most 128 MiB of HBM per device.

v0:
```python
import functools
import math

import jax
import jax.numpy as jnp
import numpy as np
from jax import lax
from jax.experimental import pallas as pl
from jax.experimental.pallas import tpu as pltpu
from jax.sharding import PartitionSpec as P

MESH = pl.DeviceIdType.MESH
PAIR = 16


def wait_all(copies):
    for copy in copies:
        copy.wait()


def lines_of(coefs, groups):
    real, imag = coefs
    blocks, wide = real.shape
    block = wide // (2 * groups)
    span = 2 * block
    modes = block // PAIR
    lane = lax.broadcasted_iota(jnp.int32, (blocks, span), 1)
    whole = lax.broadcasted_iota(jnp.int32, (blocks, wide), 1)

    def partners(x):
        moved = pltpu.roll(x, wide - modes, 1)
        middle = pltpu.roll(x, wide // 2 - modes, 1)
        return jnp.where(whole >= wide - modes, middle, moved)

    mates = [partners(real), partners(imag)]
    low = lane < block
    out = []
    for g in range(groups):
        own = g // 2 * span
        mate = (2 * groups - 1 - g) // 2 * span
        d = [x[:, own : own + span] for x in (real, imag)]
        p = [x[:, mate : mate + span] for x in mates]
        if g % 2:
            d = [pltpu.roll(x, block, 1) for x in d]
            p = [pltpu.roll(x, block, 1) for x in p]
        first = lane < modes
        last = lane >= span - modes
        re0, re1 = jnp.where(low, d[0], p[0]), jnp.where(low, -d[1], -p[1])
        im0, im1 = jnp.where(low, d[1], -p[1]), jnp.where(low, d[0], -p[0])
        if g == 0:
            im0 = jnp.where(first, 0.0, jnp.where(last, re0, im0))
            im1 = jnp.where(first, 0.0, jnp.where(last, re1, im1))
            re0 = jnp.where(last, 0.0, re0)
            re1 = jnp.where(last, 0.0, re1)
        out.append((jnp.concatenate([re0, re1], axis=1), jnp.concatenate([im0, im1], axis=1)))
    return out


def spread_mask(depth, modes):
    span = depth // 2
    lane = lax.broadcasted_iota(jnp.int32, (PAIR, depth), 1) % span
    kept = jnp.where(lane < span // 2, lane // modes, (span - 1 - lane) // modes)
    return kept == lax.broadcasted_iota(jnp.int32, (PAIR, depth), 0)


def stack_modes(ref, chunk, g, length):
    pieces = []
    for c in range(2):
        for start in (PAIR * g, length + 1 - PAIR * (g + 1)):
            block = ref[chunk, c, pl.ds(start, PAIR)]
            pieces.append(block.reshape(PAIR * block.shape[1], block.shape[2]))
    return jnp.concatenate(pieces, axis=0)


def rebuild(left, modes, mid_ref, g):
    rebuilt = jnp.dot(left, modes, preferred_element_type=jnp.float32).astype(jnp.bfloat16)
    for b in range(mid_ref.shape[0]):
        mid_ref[b, pl.ds(g * 2 * PAIR, 2 * PAIR)] = rebuilt[b * 2 * PAIR : (b + 1) * 2 * PAIR]


def gather_kernel(
    n_freq, n_space, group, parts, factor, early,
    spectra_ref, eigvecs_ref, weights_ref, basis_hbm, *refs,
):
    early_ref = refs[0] if early else None
    (
        late_ref, left_ref, taken, sbuf, ebuf, wbuf, wide, acc, pieces, land, own, quad, every,
        line_ref, mid_ref, carry_ref, basis_ref,
        send_a, recv_a, local_sem, s_sem, e_sem, w_sem, send_1, recv_1, send_2, recv_2, send_3, recv_3,
    ) = refs[1 if early else 0 :]
    f = lax.axis_index("freq")
    s = lax.axis_index("space")
    _, count, modes, points = eigvecs_ref.shape
    chunks, _, length1, _, tile = taken.shape
    length = length1 - 1
    width = points // n_freq
    blocks = acc.shape[1]
    half = group * modes
    halves = count // group
    groups = length // (2 * PAIR)
    cut = points // parts
    steps = halves * parts

    barrier = pltpu.get_barrier_semaphore()
    for df in range(1, n_freq):
        pl.semaphore_signal(barrier, inc=1, device_id=(lax.rem(f + df, n_freq), s), device_id_type=MESH)
    for ds in range(1, n_space):
        pl.semaphore_signal(barrier, inc=1, device_id=(f, lax.rem(s + ds, n_space)), device_id_type=MESH)

    def fetch(step, slot):
        h, i = step // parts, step % parts
        column = pl.multiple_of(i * cut, cut)
        return [
            pltpu.make_async_copy(
                spectra_ref.at[:, pl.ds(pl.multiple_of(h * (group * blocks), group * blocks), group * blocks), pl.ds(column, cut)],
                sbuf.at[slot], s_sem.at[slot],
            ),
            pltpu.make_async_copy(
                eigvecs_ref.at[:, pl.ds(h * group, group), :, pl.ds(column, cut)], ebuf.at[slot], e_sem.at[slot]
            ),
        ]

    for copy in fetch(0, 0):
        copy.start()
    small = [
        pltpu.make_async_copy(weights_ref, wbuf, w_sem.at[0]),
        pltpu.make_async_copy(basis_hbm, basis_ref, w_sem.at[1]),
    ]
    for copy in small:
        copy.start()

    def swap(j, c, df):
        target = lax.rem(f + df, n_freq)
        column = pl.multiple_of(target * width + j * tile, tile)
        return pltpu.make_async_remote_copy(
            src_ref=eigvecs_ref.at[c, :, :, pl.ds(column, tile)],
            dst_ref=taken.at[j, c, pl.ds(f * count, count)],
            send_sem=send_a.at[j, c, df], recv_sem=recv_a.at[j, c, df],
            device_id=(target, s), device_id_type=MESH,
        )

    def keep(j, c):
        column = pl.multiple_of(f * width + j * tile, tile)
        return pltpu.make_async_copy(
            eigvecs_ref.at[c, :, :, pl.ds(column, tile)], taken.at[j, c, pl.ds(f * count, count)], local_sem.at[j, c]
        )

    order = [(j, c) for j in range(chunks) for c in range(2)]
    ahead = len(order) // 2
    pl.semaphore_wait(barrier, n_freq + n_space - 2)
    for j, c in order[:ahead]:
        for df in range(1, n_freq):
            swap(j, c, df).start()
    for j, c in order:
        keep(j, c).start()

    wait_all(small)
    for i in range(parts):
        wide[i] = wbuf[i * cut : (i + 1) * cut].astype(jnp.float32).reshape(1, cut)
    acc[...] = jnp.zeros_like(acc)
    owner = lax.broadcasted_iota(jnp.int32, (blocks, 2 * half), 1) % half // modes

    def project(step, carry):
        slot = lax.rem(step, 2)

        @pl.when(step + 1 < steps)
        def _():
            for copy in fetch(step + 1, lax.rem(step + 1, 2)):
                copy.start()

        wait_all(fetch(step, slot))
        h, i = step // parts, step % parts
        weights = wide[i]
        weighted = jnp.concatenate(
            [
                (ebuf[slot, c].reshape(half, cut).astype(jnp.float32) * weights).astype(jnp.bfloat16)
                for c in range(2)
            ],
            axis=0,
        )
        for c in range(2):
            product = lax.dot_general(
                sbuf[slot, c], weighted, (((1,), (1,)), ((), ())), preferred_element_type=jnp.float32
            )
            total = acc[2 * h + c]
            for j in range(group):
                total += jnp.where(owner == j, product[j * blocks : (j + 1) * blocks], 0.0)
            acc[2 * h + c] = total
        return carry

    lax.fori_loop(0, steps, project, 0)

    rows = pieces.shape[1]
    split = blocks // rows
    for h in range(halves):
        a, b = acc[2 * h], acc[2 * h + 1]
        both = (a[:, :half] + b[:, half:], b[:, :half] - a[:, half:])
        for c in range(2):
            for q in range(split):
                pieces[(2 * h + c) * split + q] = both[c][q * rows : (q + 1) * rows]

    first = []
    for ds in range(1, n_space):
        target = lax.rem(s + ds, n_space)
        first.append(
            pltpu.make_async_remote_copy(
                src_ref=pieces.at[target], dst_ref=land.at[ds], send_sem=send_1.at[ds], recv_sem=recv_1.at[ds],
                device_id=(f, target), device_id_type=MESH,
            )
        )
        first[-1].start()
    total = pieces[s]
    for ds in range(1, n_space):
        first[ds - 1].wait_recv()
        total += land[ds]
    own[...] = total
    second = []
    for df in range(1, n_freq):
        second.append(
            pltpu.make_async_remote_copy(
                src_ref=own, dst_ref=quad.at[f], send_sem=send_2.at[df], recv_sem=recv_2.at[df],
                device_id=(lax.rem(f + df, n_freq), s), device_id_type=MESH,
            )
        )
        second[-1].start()
    for j, c in order[ahead:]:
        for df in range(1, n_freq):
            swap(j, c, df).start()
    quad[f] = total
    for copy in second:
        copy.wait_recv()
    third = []
    for ds in range(1, n_space):
        third.append(
            pltpu.make_async_remote_copy(
                src_ref=quad, dst_ref=every.at[s], send_sem=send_3.at[ds], recv_sem=recv_3.at[ds],
                device_id=(f, lax.rem(s + ds, n_space)), device_id_type=MESH,
            )
        )
        third[-1].start()
    every[s] = quad[...]
    for copy in third:
        copy.wait_recv()

    coefs = []
    for c in range(2):
        lanes = []
        for g in range(n_freq):
            for h in range(halves):
                base = (2 * h + c) * split
                lanes.append(jnp.concatenate([every[base + q, g] for q in range(split)], axis=0))
        coefs.append(jnp.concatenate(lanes, axis=1) * factor)
    for g, pair in enumerate(lines_of(coefs, groups)):
        for c in range(2):
            line_ref[g, c] = pair[c]
    mask = spread_mask(left_ref.shape[2], modes)

    def fill(g, carry):
        for c in range(2):
            lines = line_ref[g, c]
            for b in range(blocks):
                left_ref[g, (2 * b + c) * PAIR : (2 * b + c + 1) * PAIR] = jnp.where(
                    mask, lines[b : b + 1], 0.0
                ).astype(jnp.bfloat16)
        return carry

    lax.fori_loop(0, groups, fill, 0)

    def arrived(j):
        for c in range(2):
            keep(j, c).wait()
            for df in range(1, n_freq):
                swap(j, c, df).wait_recv()
        for c in range(2):
            taken[j, c, length] = taken[j, c, length // 2]

    half_length = length // 2

    def finish(j, carry):
        arrived(j)

        def one(g, inner):
            rebuild(left_ref[g], stack_modes(taken, j, g, length), mid_ref, g)
            return inner

        lax.fori_loop(0, groups, one, 0)
        carry_ref[...] = jnp.zeros_like(carry_ref)

        def add(b, inner):
            series = jnp.dot(basis_ref[...], mid_ref[b], preferred_element_type=jnp.float32)
            early_ref[j, pl.ds(pl.multiple_of(b * half_length, half_length), half_length)] = (
                series[:half_length] + carry_ref[...]
            )
            carry_ref[...] = series[half_length:]
            return inner

        lax.fori_loop(0, blocks, add, 0)
        early_ref[j, blocks * half_length :] = carry_ref[...]
        return carry

    if early:
        lax.fori_loop(0, early, finish, 0)
    for j in range(early, chunks):
        arrived(j)

        def arrange(g, carry):
            late_ref[j - early, g] = stack_modes(taken, j, g, length)
            return carry

        lax.fori_loop(0, groups, arrange, 0)
    for copy in first + second + third:
        copy.wait_send()
    for j, c in order:
        for df in range(1, n_freq):
            swap(j, c, df).wait_send()


def gather(spectra, eigvecs, weights, basis, n_freq, n_space, blocks, factor, tile, early):
    _, count, modes, points = eigvecs.shape
    length = n_freq * count
    group = min(2 * PAIR, count)
    half = group * modes
    halves = count // group
    width = points // n_freq
    chunks = width // tile
    parts = 4
    cut = points // parts
    groups = length // (2 * PAIR)
    depth = 4 * PAIR * modes
    rows = halves * 2 * blocks // n_space
    out_rows = (blocks + 1) * (length // 2)
    hbm = pl.BlockSpec(memory_space=pltpu.HBM)
    vmem = pl.BlockSpec(memory_space=pltpu.VMEM)
    out_shape = [
        jax.ShapeDtypeStruct((chunks - early, groups, depth, tile), jnp.bfloat16),
        jax.ShapeDtypeStruct((groups, blocks * 2 * PAIR, depth), jnp.bfloat16),
    ]
    if early:
        out_shape = [jax.ShapeDtypeStruct((early, out_rows, tile), jnp.float32)] + out_shape
    dma = pltpu.SemaphoreType.DMA
    return pl.pallas_call(
        functools.partial(gather_kernel, n_freq, n_space, group, parts, factor, early),
        out_shape=out_shape,
        in_specs=[hbm] * 4,
        out_specs=[vmem] * len(out_shape),
        scratch_shapes=[
            pltpu.VMEM((chunks, 2, length + 1, modes, tile), jnp.bfloat16),
            pltpu.VMEM((2, 2, group * blocks, cut), jnp.bfloat16),
            pltpu.VMEM((2, 2, group, modes, cut), jnp.bfloat16),
            pltpu.VMEM((points,), jnp.bfloat16),
            pltpu.VMEM((parts, 1, cut), jnp.float32),
            pltpu.VMEM((2 * halves, blocks, 2 * half), jnp.float32),
            pltpu.VMEM((n_space, rows, half), jnp.float32),
            pltpu.VMEM((n_space, rows, half), jnp.float32),
            pltpu.VMEM((rows, half), jnp.float32),
            pltpu.VMEM((n_freq, rows, half), jnp.float32),
            pltpu.VMEM((n_space, n_freq, rows, half), jnp.float32),
            pltpu.VMEM((groups, 2, blocks, depth), jnp.float32),
            pltpu.VMEM((blocks, length, tile), jnp.bfloat16),
            pltpu.VMEM((length // 2, tile), jnp.float32),
            pltpu.VMEM((length, length), jnp.bfloat16),
            dma((chunks, 2, n_freq)),
            dma((chunks, 2, n_freq)),
            dma((chunks, 2)),
            dma((2,)),
            dma((2,)),
            dma((2,)),
            dma((n_space,)),
            dma((n_space,)),
            dma((n_freq,)),
            dma((n_freq,)),
            dma((n_space,)),
            dma((n_space,)),
        ],
        compiler_params=pltpu.CompilerParams(
            collective_id=0, has_side_effects=True, vmem_limit_bytes=32 << 20
        ),
        cost_estimate=pl.CostEstimate(
            flops=8 * spectra.shape[1] * points * 2 * half, bytes_accessed=4 * spectra.size, transcendentals=0
        ),
        name="gather",
    )(*[pltpu.with_memory_space_constraint(x, pltpu.HBM) for x in (spectra, eigvecs, weights, basis)])


def finish_kernel(early, tile, *refs):
    if early:
        early_ref, refs = refs[0], refs[1:]
    late_ref, left_ref, basis_ref, out_ref, mid_ref, result, copy_sem, late_sem = refs
    blocks, length, _ = mid_ref.shape
    groups = left_ref.shape[0]
    half_length = length // 2
    runs = late_sem.shape[1]
    copies = []
    for j in range(early):
        copies.append(
            pltpu.make_async_copy(early_ref.at[j], out_ref.at[:, j * tile : (j + 1) * tile], copy_sem.at[j])
        )
        copies[-1].start()
    for l in range(late_ref.shape[0]):
        for g in range(groups):
            rebuild(left_ref[g], late_ref[l, g], mid_ref, g)
        carry = None
        done = 0
        for b in range(blocks):
            series = jnp.dot(basis_ref[...], mid_ref[b], preferred_element_type=jnp.float32)
            lead = series[:half_length]
            result[l, b * half_length : (b + 1) * half_length] = lead if carry is None else lead + carry
            carry = series[half_length:]
            last = b == blocks - 1
            if last:
                result[l, blocks * half_length :] = carry
            if last or (b + 1) % (blocks // runs) == 0:
                stop = (b + 1 + last) * half_length
                column = (early + l) * tile
                copies.append(
                    pltpu.make_async_copy(
                        result.at[l, done:stop], out_ref.at[done:stop, column : column + tile],
                        late_sem.at[l, (b + 1) // (blocks // runs) - 1],
                    )
                )
                copies[-1].start()
                done = stop
    wait_all(copies)


def finish(arrays, basis, blocks, length, width, tile, early):
    late, left = arrays[-2:]
    out_rows = (blocks + 1) * (length // 2)
    vmem = pl.BlockSpec(memory_space=pltpu.VMEM)
    runs = 4
    return pl.pallas_call(
        functools.partial(finish_kernel, early, tile),
        out_shape=jax.ShapeDtypeStruct((out_rows, width), jnp.float32),
        in_specs=[vmem] * (len(arrays) + 1),
        out_specs=pl.BlockSpec(memory_space=pltpu.HBM),
        scratch_shapes=[
            pltpu.VMEM((blocks, length, tile), jnp.bfloat16),
            pltpu.VMEM((late.shape[0], out_rows, tile), jnp.float32),
            pltpu.SemaphoreType.DMA((max(early, 1),)),
            pltpu.SemaphoreType.DMA((late.shape[0], runs)),
        ],
        compiler_params=pltpu.CompilerParams(vmem_limit_bytes=24 << 20),
        cost_estimate=pl.CostEstimate(
            flops=4 * length * length * blocks * tile, bytes_accessed=4 * out_rows * width, transcendentals=0
        ),
        name="finish",
    )(*arrays, basis)


def basis_of(length):
    groups = length // (2 * PAIR)
    freq = np.arange(length // 2).reshape(groups, 1, PAIR)
    time = np.arange(length).reshape(length, 1, 1, 1)
    phase = 2.0 * np.pi * ((freq * time) % length) / length
    both = np.concatenate([np.cos(phase), -np.sin(phase)], axis=2)
    both[:, 0, 1, 0] = 1.0 - 2.0 * (np.arange(length) % 2)
    window = np.sin(np.pi * (np.arange(length) + 0.5) / length) / math.sqrt(length)
    return jnp.asarray((both.reshape(length, length) * window[:, None]).astype(np.float32)).astype(jnp.bfloat16)


def body(spectra, eigvecs, weights):
    n_freq = lax.axis_size("freq")
    n_space = lax.axis_size("space")
    _, count, blocks, points = spectra.shape
    factor = 1.0 / math.sqrt(points * n_space)
    length = n_freq * count
    width = points // n_freq
    tile = 256 if width % 256 == 0 else width
    early = width // tile - 1
    basis = basis_of(length)
    spectra = spectra.reshape(2, count * blocks, points)
    arrays = gather(spectra, eigvecs, weights, basis, n_freq, n_space, blocks, factor, tile, early)
    return finish(arrays, basis, blocks, length, width, tile, early)


def solution(mesh):
    placed = (P(None, "freq", None, "space"), P(None, "freq", None, "space"), P("space"))
    return jax.shard_map(
        body, mesh=mesh, in_specs=placed, out_specs=P(None, ("space", "freq")), check_vma=False
    )
```

profile of v0, /device:TPU:0, one launch (start us, length us, event | category | flops | bytes accessed | tf_op | source)
XLA Modules:
  0.0 64.1 jit_solution(7689640931941549092)
XLA Ops:
  0.0 0.0 copy-start
  0.0 57.8 %gather.1 = (f32[3,3200,256]{2,1,0:T(8,128)S(1)}, bf16[1,8,256,256]{3,2,1,0:T(8,128)(2,1)S(1)}, bf16[8,768,256]{2,1,0:T(8,128)(2,1)S(1)}) custom-call(bf16[2,1536,4096]{2,1,0:T(8,128)(2,1)} %bitcast.1, bf16[2,64,4,4096]{3,2,1,0:T(4,128)(2,1)} %eigvecs_ref.1, bf16[4096]{0:T(1024)(128)(2,1)} %weights_ref.1, bf16[256,256]{1,0:T(8,128)(2,1)} %constant.3.basis_hbm.refs_3_), custom_call_target="tpu_custom_call" | custom-call | flops 12884901888 | bytes 50331648 | tf_op jit(solution)/shard_map/gather/pallas_call | solution.py:341
  57.8 0.0 copy-done
  57.8 6.2 %finish.1 = f32[3200,1024]{1,0:T(8,128)} custom-call(f32[3,3200,256]{2,1,0:T(8,128)S(1)} %get-tuple-element.8.refs_0_, bf16[1,8,256,256]{3,2,1,0:T(8,128)(2,1)S(1)} %get-tuple-element.9.refs_1_, bf16[8,768,256]{2,1,0:T(8,128)(2,1)S(1)} %get-tuple-element.10.refs_2_, bf16[256,256]{1,0:T(8,128)(2,1)S(1)} %copy-done), custom_call_target="tpu_custom_call" | custom-call | flops 1610612736 | bytes 13107200 | tf_op jit(solution)/shard_map/finish/pallas_call | solution.py:431
Async XLA Ops:
  0.0 57.8 %copy-start = (bf16[256,256]{1,0:T(8,128)(2,1)S(1)}, bf16[256,256]{1,0:T(8,128)(2,1)}, u32[]{:S(2)}) copy-start(bf16[256,256]{1,0:T(8,128)(2,1)} %constant.3.basis_hbm.refs_3_) | copy-start | bytes 393220
where the time goes:
time: 64.2 us; the launch traced here: 64.1 us
  Pallas kernels  64 us (100%)
    pallas_call x1, Pallas kernels, gather(): pl.pallas_call(functools.partial(gather_kernel, n_freq, n_space, group, p...  57.8 us
    pallas_call x1, Pallas kernels, finish(): pl.pallas_call(functools.partial(finish_kernel, early, tile), out_shape=j...  6.22 us

commit v1 on v0

--- a/solution.py
+++ b/solution.py
@@ -63,31 +63,41 @@
     return kept == lax.broadcasted_iota(jnp.int32, (PAIR, depth), 0)
 
 
-def stack_modes(ref, chunk, g, length):
+def stack_modes(ref, tiles, g, length):
     pieces = []
     for c in range(2):
         for start in (PAIR * g, length + 1 - PAIR * (g + 1)):
-            block = ref[chunk, c, pl.ds(start, PAIR)]
-            pieces.append(block.reshape(PAIR * block.shape[1], block.shape[2]))
+            blocks = [ref[tile, c, pl.ds(start, PAIR)] for tile in tiles]
+            blocks = [block.reshape(PAIR * block.shape[1], block.shape[2]) for block in blocks]
+            pieces.append(blocks[0] if len(blocks) == 1 else jnp.concatenate(blocks, axis=1))
     return jnp.concatenate(pieces, axis=0)
 
 
-def rebuild(left, modes, mid_ref, g):
-    rebuilt = jnp.dot(left, modes, preferred_element_type=jnp.float32).astype(jnp.bfloat16)
-    for b in range(mid_ref.shape[0]):
-        mid_ref[b, pl.ds(g * 2 * PAIR, 2 * PAIR)] = rebuilt[b * 2 * PAIR : (b + 1) * 2 * PAIR]
+def synthesize(modes_of, left_ref, basis_ref, mid_ref, wide, put):
+    blocks, length, _ = mid_ref.shape
+    half_length = length // 2
+    for g in range(left_ref.shape[0]):
+        rebuilt = jnp.dot(left_ref[g], modes_of(g), preferred_element_type=jnp.float32).astype(jnp.bfloat16)
+        for b in range(blocks):
+            mid_ref[b, g * 2 * PAIR : (g + 1) * 2 * PAIR, :wide] = rebuilt[b * 2 * PAIR : (b + 1) * 2 * PAIR]
+    tail = None
+    for b in range(blocks):
+        series = jnp.dot(basis_ref[...], mid_ref[b, :, :wide], preferred_element_type=jnp.float32)
+        lead = series[:half_length]
+        put(b, lead if tail is None else lead + tail)
+        tail = series[half_length:]
+    put(blocks, tail)
 
 
 def gather_kernel(
-    n_freq, n_space, group, parts, factor, early,
+    n_freq, n_space, group, parts, factor,
     spectra_ref, eigvecs_ref, weights_ref, basis_hbm, *refs,
 ):
-    early_ref = refs[0] if early else None
     (
-        late_ref, left_ref, taken, sbuf, ebuf, wbuf, wide, acc, pieces, land, own, quad, every,
-        line_ref, mid_ref, carry_ref, basis_ref,
+        early_ref, late_ref, left_ref, taken, sbuf, ebuf, wbuf, wide, acc, pieces, land, own, every,
+        line_ref, mid_ref, basis_ref,
         send_a, recv_a, local_sem, s_sem, e_sem, w_sem, send_1, recv_1, send_2, recv_2, send_3, recv_3,
-    ) = refs[1 if early else 0 :]
+    ) = refs
     f = lax.axis_index("freq")
     s = lax.axis_index("space")
     _, count, modes, points = eigvecs_ref.shape
@@ -104,8 +114,10 @@
     barrier = pltpu.get_barrier_semaphore()
     for df in range(1, n_freq):
         pl.semaphore_signal(barrier, inc=1, device_id=(lax.rem(f + df, n_freq), s), device_id_type=MESH)
-    for ds in range(1, n_space):
-        pl.semaphore_signal(barrier, inc=1, device_id=(f, lax.rem(s + ds, n_space)), device_id_type=MESH)
+    bits = [1 << i for i in range(n_space.bit_length() - 1)]
+    mates = [s + bit - 2 * bit * (s // bit % 2) for bit in bits]
+    for mate in mates:
+        pl.semaphore_signal(barrier, inc=1, device_id=(f, mate), device_id_type=MESH)
 
     def fetch(step, slot):
         h, i = step // parts, step % parts
@@ -147,7 +159,7 @@
 
     order = [(j, c) for j in range(chunks) for c in range(2)]
     ahead = len(order) // 2
-    pl.semaphore_wait(barrier, n_freq + n_space - 2)
+    pl.semaphore_wait(barrier, n_freq - 1 + len(bits))
     for j, c in order[:ahead]:
         for df in range(1, n_freq):
             swap(j, c, df).start()
@@ -199,48 +211,45 @@
             for q in range(split):
                 pieces[(2 * h + c) * split + q] = both[c][q * rows : (q + 1) * rows]
 
-    first = []
-    for ds in range(1, n_space):
-        target = lax.rem(s + ds, n_space)
-        first.append(
-            pltpu.make_async_remote_copy(
-                src_ref=pieces.at[target], dst_ref=land.at[ds], send_sem=send_1.at[ds], recv_sem=recv_1.at[ds],
-                device_id=(f, target), device_id_type=MESH,
-            )
-        )
-        first[-1].start()
-    total = pieces[s]
-    for ds in range(1, n_space):
-        first[ds - 1].wait_recv()
-        total += land[ds]
-    own[...] = total
+    started = []
+
+    def send(source, target, sems, where):
+        copy = pltpu.make_async_remote_copy(
+            src_ref=source, dst_ref=target, send_sem=sems[0], recv_sem=sems[1], device_id=where, device_id_type=MESH
+        )
+        copy.start()
+        started.append(copy)
+        return copy
+
+    base, size = 0, n_space
+    bases = []
+    for i, (bit, mate) in enumerate(zip(bits, mates)):
+        size //= 2
+        mine = base + s // bit % 2 * size
+        other = base + size - s // bit % 2 * size
+        copy = send(
+            pieces.at[pl.ds(other, size)], land.at[pl.ds(size, size)], (send_1.at[i], recv_1.at[i]), (f, mate)
+        )
+        copy.wait_recv()
+        pieces[pl.ds(mine, size)] = pieces[pl.ds(mine, size)] + land[size : 2 * size]
+        base = mine
+        bases.append((base, size))
+    own[...] = (pieces[base] * factor).astype(own.dtype)
     second = []
     for df in range(1, n_freq):
         second.append(
-            pltpu.make_async_remote_copy(
-                src_ref=own, dst_ref=quad.at[f], send_sem=send_2.at[df], recv_sem=recv_2.at[df],
-                device_id=(lax.rem(f + df, n_freq), s), device_id_type=MESH,
-            )
-        )
-        second[-1].start()
+            send(own, every.at[base, f], (send_2.at[df], recv_2.at[df]), (lax.rem(f + df, n_freq), s))
+        )
     for j, c in order[ahead:]:
         for df in range(1, n_freq):
             swap(j, c, df).start()
-    quad[f] = total
+    every[base, f] = own[...]
     for copy in second:
         copy.wait_recv()
-    third = []
-    for ds in range(1, n_space):
-        third.append(
-            pltpu.make_async_remote_copy(
-                src_ref=quad, dst_ref=every.at[s], send_sem=send_3.at[ds], recv_sem=recv_3.at[ds],
-                device_id=(f, lax.rem(s + ds, n_space)), device_id_type=MESH,
-            )
-        )
-        third[-1].start()
-    every[s] = quad[...]
-    for copy in third:
-        copy.wait_recv()
+    for i, mate in reversed(list(enumerate(mates))):
+        low, size = bases[i]
+        block = every.at[pl.ds(low, size)]
+        send(block, block, (send_3.at[i], recv_3.at[i]), (f, mate)).wait_recv()
 
     coefs = []
     for c in range(2):
@@ -248,8 +257,10 @@
         for g in range(n_freq):
             for h in range(halves):
                 base = (2 * h + c) * split
-                lanes.append(jnp.concatenate([every[base + q, g] for q in range(split)], axis=0))
-        coefs.append(jnp.concatenate(lanes, axis=1) * factor)
+                lanes.append(
+                    jnp.concatenate([every[base + q, g].astype(jnp.float32) for q in range(split)], axis=0)
+                )
+        coefs.append(jnp.concatenate(lanes, axis=1))
     for g, pair in enumerate(lines_of(coefs, groups)):
         for c in range(2):
             line_ref[g, c] = pair[c]
@@ -276,46 +287,46 @@
 
     half_length = length // 2
 
+    def put_at(column, wide):
+        def put(b, rows):
+            early_ref[b * half_length : (b + 1) * half_length, pl.ds(column, wide)] = rows
+
+        return put
+
     def finish(j, carry):
-        arrived(j)
-
-        def one(g, inner):
-            rebuild(left_ref[g], stack_modes(taken, j, g, length), mid_ref, g)
-            return inner
-
-        lax.fori_loop(0, groups, one, 0)
-        carry_ref[...] = jnp.zeros_like(carry_ref)
-
-        def add(b, inner):
-            series = jnp.dot(basis_ref[...], mid_ref[b], preferred_element_type=jnp.float32)
-            early_ref[j, pl.ds(pl.multiple_of(b * half_length, half_length), half_length)] = (
-                series[:half_length] + carry_ref[...]
-            )
-            carry_ref[...] = series[half_length:]
-            return inner
-
-        lax.fori_loop(0, blocks, add, 0)
-        early_ref[j, blocks * half_length :] = carry_ref[...]
+        tiles = (2 * j, 2 * j + 1)
+        for one in tiles:
+            arrived(one)
+        synthesize(
+            lambda g: stack_modes(taken, tiles, g, length), left_ref, basis_ref, mid_ref, 2 * tile,
+            put_at(pl.multiple_of(j * 2 * tile, 2 * tile), 2 * tile),
+        )
         return carry
 
-    if early:
-        lax.fori_loop(0, early, finish, 0)
-    for j in range(early, chunks):
-        arrived(j)
-
-        def arrange(g, carry):
-            late_ref[j - early, g] = stack_modes(taken, j, g, length)
-            return carry
-
-        lax.fori_loop(0, groups, arrange, 0)
-    for copy in first + second + third:
+    early = chunks - 1
+    if early >= 2:
+        lax.fori_loop(0, early // 2, finish, 0)
+    if early % 2:
+        arrived(early - 1)
+        synthesize(
+            lambda g: stack_modes(taken, (early - 1,), g, length), left_ref, basis_ref, mid_ref, tile,
+            put_at((early - 1) * tile, tile),
+        )
+    arrived(early)
+
+    def arrange(g, carry):
+        late_ref[g] = stack_modes(taken, (early,), g, length)
+        return carry
+
+    lax.fori_loop(0, groups, arrange, 0)
+    for copy in started:
         copy.wait_send()
     for j, c in order:
         for df in range(1, n_freq):
             swap(j, c, df).wait_send()
 
 
-def gather(spectra, eigvecs, weights, basis, n_freq, n_space, blocks, factor, tile, early):
+def gather(spectra, eigvecs, weights, basis, n_freq, n_space, blocks, factor, tile):
     _, count, modes, points = eigvecs.shape
     length = n_freq * count
     group = min(2 * PAIR, count)
@@ -332,14 +343,13 @@
     hbm = pl.BlockSpec(memory_space=pltpu.HBM)
     vmem = pl.BlockSpec(memory_space=pltpu.VMEM)
     out_shape = [
-        jax.ShapeDtypeStruct((chunks - early, groups, depth, tile), jnp.bfloat16),
+        jax.ShapeDtypeStruct((out_rows, width - tile), jnp.float32),
+        jax.ShapeDtypeStruct((groups, depth, tile), jnp.bfloat16),
         jax.ShapeDtypeStruct((groups, blocks * 2 * PAIR, depth), jnp.bfloat16),
     ]
-    if early:
-        out_shape = [jax.ShapeDtypeStruct((early, out_rows, tile), jnp.float32)] + out_shape
     dma = pltpu.SemaphoreType.DMA
     return pl.pallas_call(
-        functools.partial(gather_kernel, n_freq, n_space, group, parts, factor, early),
+        functools.partial(gather_kernel, n_freq, n_space, group, parts, factor),
         out_shape=out_shape,
         in_specs=[hbm] * 4,
         out_specs=[vmem] * len(out_shape),
@@ -352,12 +362,10 @@
             pltpu.VMEM((2 * halves, blocks, 2 * half), jnp.float32),
             pltpu.VMEM((n_space, rows, half), jnp.float32),
             pltpu.VMEM((n_space, rows, half), jnp.float32),
-            pltpu.VMEM((rows, half), jnp.float32),
-            pltpu.VMEM((n_freq, rows, half), jnp.float32),
-            pltpu.VMEM((n_space, n_freq, rows, half), jnp.float32),
+            pltpu.VMEM((rows, half), jnp.bfloat16),
+            pltpu.VMEM((n_space, n_freq, rows, half), jnp.bfloat16),
             pltpu.VMEM((groups, 2, blocks, depth), jnp.float32),
-            pltpu.VMEM((blocks, length, tile), jnp.bfloat16),
-            pltpu.VMEM((length // 2, tile), jnp.float32),
+            pltpu.VMEM((blocks, length, 2 * tile), jnp.bfloat16),
             pltpu.VMEM((length, length), jnp.bfloat16),
             dma((chunks, 2, n_freq)),
             dma((chunks, 2, n_freq)),
@@ -382,62 +390,44 @@
     )(*[pltpu.with_memory_space_constraint(x, pltpu.HBM) for x in (spectra, eigvecs, weights, basis)])
 
 
-def finish_kernel(early, tile, *refs):
-    if early:
-        early_ref, refs = refs[0], refs[1:]
-    late_ref, left_ref, basis_ref, out_ref, mid_ref, result, copy_sem, late_sem = refs
-    blocks, length, _ = mid_ref.shape
-    groups = left_ref.shape[0]
+def finish_kernel(early_ref, late_ref, left_ref, basis_ref, out_ref, mid_ref, result, early_sem, late_sem):
+    blocks, length, tile = mid_ref.shape
     half_length = length // 2
-    runs = late_sem.shape[1]
-    copies = []
-    for j in range(early):
-        copies.append(
-            pltpu.make_async_copy(early_ref.at[j], out_ref.at[:, j * tile : (j + 1) * tile], copy_sem.at[j])
-        )
-        copies[-1].start()
-    for l in range(late_ref.shape[0]):
-        for g in range(groups):
-            rebuild(left_ref[g], late_ref[l, g], mid_ref, g)
-        carry = None
-        done = 0
-        for b in range(blocks):
-            series = jnp.dot(basis_ref[...], mid_ref[b], preferred_element_type=jnp.float32)
-            lead = series[:half_length]
-            result[l, b * half_length : (b + 1) * half_length] = lead if carry is None else lead + carry
-            carry = series[half_length:]
-            last = b == blocks - 1
-            if last:
-                result[l, blocks * half_length :] = carry
-            if last or (b + 1) % (blocks // runs) == 0:
-                stop = (b + 1 + last) * half_length
-                column = (early + l) * tile
-                copies.append(
-                    pltpu.make_async_copy(
-                        result.at[l, done:stop], out_ref.at[done:stop, column : column + tile],
-                        late_sem.at[l, (b + 1) // (blocks // runs) - 1],
-                    )
-                )
-                copies[-1].start()
-                done = stop
+    rest = early_ref.shape[1]
+    runs = late_sem.shape[0]
+    copies = [pltpu.make_async_copy(early_ref, out_ref.at[:, :rest], early_sem)]
+    copies[0].start()
+
+    def put(b, rows):
+        result[b * half_length : (b + 1) * half_length] = rows
+        count = b + 1 if b < blocks - 1 else b
+        if b != blocks - 1 and count % (blocks // runs) == 0:
+            run = count // (blocks // runs) - 1
+            start = run * (blocks // runs) * half_length
+            span = slice(start, (b + 1) * half_length)
+            copies.append(
+                pltpu.make_async_copy(result.at[span], out_ref.at[span, rest : rest + tile], late_sem.at[run])
+            )
+            copies[-1].start()
+
+    synthesize(lambda g: late_ref[g], left_ref, basis_ref, mid_ref, tile, put)
     wait_all(copies)
 
 
-def finish(arrays, basis, blocks, length, width, tile, early):
-    late, left = arrays[-2:]
+def finish(arrays, basis, blocks, length, width, tile):
     out_rows = (blocks + 1) * (length // 2)
     vmem = pl.BlockSpec(memory_space=pltpu.VMEM)
     runs = 4
     return pl.pallas_call(
-        functools.partial(finish_kernel, early, tile),
+        finish_kernel,
         out_shape=jax.ShapeDtypeStruct((out_rows, width), jnp.float32),
         in_specs=[vmem] * (len(arrays) + 1),
         out_specs=pl.BlockSpec(memory_space=pltpu.HBM),
         scratch_shapes=[
             pltpu.VMEM((blocks, length, tile), jnp.bfloat16),
-            pltpu.VMEM((late.shape[0], out_rows, tile), jnp.float32),
-            pltpu.SemaphoreType.DMA((max(early, 1),)),
-            pltpu.SemaphoreType.DMA((late.shape[0], runs)),
+            pltpu.VMEM((out_rows, tile), jnp.float32),
+            pltpu.SemaphoreType.DMA,
+            pltpu.SemaphoreType.DMA((runs,)),
         ],
         compiler_params=pltpu.CompilerParams(vmem_limit_bytes=24 << 20),
         cost_estimate=pl.CostEstimate(
@@ -465,12 +455,11 @@
     factor = 1.0 / math.sqrt(points * n_space)
     length = n_freq * count
     width = points // n_freq
-    tile = 256 if width % 256 == 0 else width
-    early = width // tile - 1
+    tile = 128
     basis = basis_of(length)
     spectra = spectra.reshape(2, count * blocks, points)
-    arrays = gather(spectra, eigvecs, weights, basis, n_freq, n_space, blocks, factor, tile, early)
-    return finish(arrays, basis, blocks, length, width, tile, early)
+    arrays = gather(spectra, eigvecs, weights, basis, n_freq, n_space, blocks, factor, tile)
+    return finish(arrays, basis, blocks, length, width, tile)
 
 
 def solution(mesh):

time: 64.2 us -> 58.6 us (0.913)
  Pallas kernels: 64 us -> 58.5 us
    pallas_call x1, Pallas kernels: 57.8 us -> 53.5 us  [gather(): pl.pallas_call(functools.partial(gather_kernel, n_freq, n_space, group, p...]
    pallas_call x1, Pallas kernels: 6.22 us -> 4.95 us  [finish(): pl.pallas_call(finish_kernel, out_shape=jax.ShapeDtypeStruct((out_rows, w...]
where the time goes in v1:
time: 58.6 us; the launch traced here: 58.5 us
  Pallas kernels  58.5 us (100%)
    pallas_call x1, Pallas kernels, gather(): pl.pallas_call(functools.partial(gather_kernel, n_freq, n_space, group, p...  53.5 us
    pallas_call x1, Pallas kernels, finish(): pl.pallas_call(finish_kernel, out_shape=jax.ShapeDtypeStruct((out_rows, w...  4.95 us

profile of v1, /device:TPU:0, one launch (start us, length us, event | category | flops | bytes accessed | tf_op | source)
XLA Modules:
  0.0 58.5 jit_solution(7201784129238806518)
XLA Ops:
  0.0 0.0 copy-start
  0.0 53.5 %gather.1 = (f32[3200,896]{1,0:T(8,128)S(1)}, bf16[8,256,128]{2,1,0:T(8,128)(2,1)S(1)}, bf16[8,768,256]{2,1,0:T(8,128)(2,1)S(1)}) custom-call(bf16[2,1536,4096]{2,1,0:T(8,128)(2,1)} %bitcast.1, bf16[2,64,4,4096]{3,2,1,0:T(4,128)(2,1)} %eigvecs_ref.1, bf16[4096]{0:T(1024)(128)(2,1)} %weights_ref.1, bf16[256,256]{1,0:T(8,128)(2,1)} %constant.3.basis_hbm.basis_ref), custom_call_target="tpu_custom_call" | custom-call | flops 12884901888 | bytes 50331648 | tf_op jit(solution)/shard_map/gather/pallas_call | solution.py:351
  53.5 0.0 copy-done
  53.5 5.0 %finish.1 = f32[3200,1024]{1,0:T(8,128)} custom-call(f32[3200,896]{1,0:T(8,128)S(1)} %get-tuple-element.8.early_ref, bf16[8,256,128]{2,1,0:T(8,128)(2,1)S(1)} %get-tuple-element.9.late_ref, bf16[8,768,256]{2,1,0:T(8,128)(2,1)S(1)} %get-tuple-element.10.left_ref, bf16[256,256]{1,0:T(8,128)(2,1)S(1)} %copy-done), custom_call_target="tpu_custom_call" | custom-call | flops 805306368 | bytes 13107200 | tf_op jit(solution)/shard_map/finish/pallas_call | solution.py:421
Async XLA Ops:
  0.0 53.5 %copy-start = (bf16[256,256]{1,0:T(8,128)(2,1)S(1)}, bf16[256,256]{1,0:T(8,128)(2,1)}, u32[]{:S(2)}) copy-start(bf16[256,256]{1,0:T(8,128)(2,1)} %constant.3.basis_hbm.basis_ref) | copy-start | bytes 393220

commit v2 on v1

--- a/solution.py
+++ b/solution.py
@@ -11,6 +11,7 @@
 
 MESH = pl.DeviceIdType.MESH
 PAIR = 16
+AHEAD = 9
 
 
 def wait_all(copies):
@@ -63,13 +64,12 @@
     return kept == lax.broadcasted_iota(jnp.int32, (PAIR, depth), 0)
 
 
-def stack_modes(ref, tiles, g, length):
+def stack_modes(ref, tile, g, length):
     pieces = []
     for c in range(2):
         for start in (PAIR * g, length + 1 - PAIR * (g + 1)):
-            blocks = [ref[tile, c, pl.ds(start, PAIR)] for tile in tiles]
-            blocks = [block.reshape(PAIR * block.shape[1], block.shape[2]) for block in blocks]
-            pieces.append(blocks[0] if len(blocks) == 1 else jnp.concatenate(blocks, axis=1))
+            block = ref[tile, c, pl.ds(start, PAIR)]
+            pieces.append(block.reshape(PAIR * block.shape[1], block.shape[2]))
     return jnp.concatenate(pieces, axis=0)
 
 
@@ -90,19 +90,19 @@
 
 
 def gather_kernel(
-    n_freq, n_space, group, parts, factor,
+    n_freq, n_space, group, parts, factor, wides,
     spectra_ref, eigvecs_ref, weights_ref, basis_hbm, *refs,
 ):
     (
-        early_ref, late_ref, left_ref, taken, sbuf, ebuf, wbuf, wide, acc, pieces, land, own, every,
+        early_ref, late_ref, left_ref, broad, narrow, sbuf, ebuf, wbuf, wide, acc, pieces, land, below, above, upward, downward, own, every,
         line_ref, mid_ref, basis_ref,
-        send_a, recv_a, local_sem, s_sem, e_sem, w_sem, send_1, recv_1, send_2, recv_2, send_3, recv_3,
+        send_b, recv_b, send_n, recv_n, local_b, local_n, s_sem, e_sem, w_sem, send_1, recv_1, send_2, recv_2, send_3, recv_3,
     ) = refs
     f = lax.axis_index("freq")
     s = lax.axis_index("space")
     _, count, modes, points = eigvecs_ref.shape
-    chunks, _, length1, _, tile = taken.shape
-    length = length1 - 1
+    narrows, _, length, _, tile = narrow.shape
+    length -= 1
     width = points // n_freq
     blocks = acc.shape[1]
     half = group * modes
@@ -114,10 +114,17 @@
     barrier = pltpu.get_barrier_semaphore()
     for df in range(1, n_freq):
         pl.semaphore_signal(barrier, inc=1, device_id=(lax.rem(f + df, n_freq), s), device_id_type=MESH)
-    bits = [1 << i for i in range(n_space.bit_length() - 1)]
-    mates = [s + bit - 2 * bit * (s // bit % 2) for bit in bits]
-    for mate in mates:
-        pl.semaphore_signal(barrier, inc=1, device_id=(f, mate), device_id_type=MESH)
+    z, top = s // 2, n_space // 2 - 1
+    mate = s + 1 - 2 * (s % 2)
+    pl.semaphore_signal(barrier, inc=1, device_id=(f, mate), device_id_type=MESH)
+
+    @pl.when(z > 0)
+    def _():
+        pl.semaphore_signal(barrier, inc=1, device_id=(f, s - 2), device_id_type=MESH)
+
+    @pl.when(z < top)
+    def _():
+        pl.semaphore_signal(barrier, inc=1, device_id=(f, s + 2), device_id_type=MESH)
 
     def fetch(step, slot):
         h, i = step // parts, step % parts
@@ -141,30 +148,54 @@
     for copy in small:
         copy.start()
 
-    def swap(j, c, df):
+    part = count // 2
+
+    def swap_broad(j, c, r, df):
         target = lax.rem(f + df, n_freq)
-        column = pl.multiple_of(target * width + j * tile, tile)
+        column = pl.multiple_of(target * width + j * 2 * tile, 2 * tile)
+        return pltpu.make_async_remote_copy(
+            src_ref=eigvecs_ref.at[c, r * part : (r + 1) * part, :, pl.ds(column, 2 * tile)],
+            dst_ref=broad.at[j, c, pl.ds(f * count + r * part, part)],
+            send_sem=send_b.at[j, c, r, df], recv_sem=recv_b.at[j, c, r, df],
+            device_id=(target, s), device_id_type=MESH,
+        )
+
+    def swap_narrow(j, c, df):
+        target = lax.rem(f + df, n_freq)
+        column = pl.multiple_of(target * width + (2 * wides + j) * tile, tile)
         return pltpu.make_async_remote_copy(
             src_ref=eigvecs_ref.at[c, :, :, pl.ds(column, tile)],
-            dst_ref=taken.at[j, c, pl.ds(f * count, count)],
-            send_sem=send_a.at[j, c, df], recv_sem=recv_a.at[j, c, df],
+            dst_ref=narrow.at[j, c, pl.ds(f * count, count)],
+            send_sem=send_n.at[j, c, df], recv_sem=recv_n.at[j, c, df],
             device_id=(target, s), device_id_type=MESH,
         )
 
-    def keep(j, c):
-        column = pl.multiple_of(f * width + j * tile, tile)
+    def keep_broad(j, c):
+        column = pl.multiple_of(f * width + j * 2 * tile, 2 * tile)
         return pltpu.make_async_copy(
-            eigvecs_ref.at[c, :, :, pl.ds(column, tile)], taken.at[j, c, pl.ds(f * count, count)], local_sem.at[j, c]
-        )
-
-    order = [(j, c) for j in range(chunks) for c in range(2)]
-    ahead = len(order) // 2
-    pl.semaphore_wait(barrier, n_freq - 1 + len(bits))
-    for j, c in order[:ahead]:
+            eigvecs_ref.at[c, :, :, pl.ds(column, 2 * tile)], broad.at[j, c, pl.ds(f * count, count)], local_b.at[j, c]
+        )
+
+    def keep_narrow(j, c):
+        column = pl.multiple_of(f * width + (2 * wides + j) * tile, tile)
+        return pltpu.make_async_copy(
+            eigvecs_ref.at[c, :, :, pl.ds(column, tile)], narrow.at[j, c, pl.ds(f * count, count)], local_n.at[j, c]
+        )
+
+    order = [
+        functools.partial(swap_broad, j, c, r) for j in range(wides) for c in range(2) for r in range(2)
+    ] + [functools.partial(swap_narrow, j, c) for j in range(narrows) for c in range(2)]
+    ahead = AHEAD * len(order) // 16
+    lower, upper = (z + top) // (top + 1), (2 * top - z) // (top + 1)
+    pl.semaphore_wait(barrier, n_freq + lower + upper)
+    for swap in order[:ahead]:
         for df in range(1, n_freq):
-            swap(j, c, df).start()
-    for j, c in order:
-        keep(j, c).start()
+            swap(df).start()
+    for c in range(2):
+        for j in range(wides):
+            keep_broad(j, c).start()
+        for j in range(narrows):
+            keep_narrow(j, c).start()
 
     wait_all(small)
     for i in range(parts):
@@ -221,35 +252,65 @@
         started.append(copy)
         return copy
 
-    base, size = 0, n_space
-    bases = []
-    for i, (bit, mate) in enumerate(zip(bits, mates)):
-        size //= 2
-        mine = base + s // bit % 2 * size
-        other = base + size - s // bit % 2 * size
-        copy = send(
-            pieces.at[pl.ds(other, size)], land.at[pl.ds(size, size)], (send_1.at[i], recv_1.at[i]), (f, mate)
-        )
-        copy.wait_recv()
-        pieces[pl.ds(mine, size)] = pieces[pl.ds(mine, size)] + land[size : 2 * size]
-        base = mine
-        bases.append((base, size))
-    own[...] = (pieces[base] * factor).astype(own.dtype)
+    size = n_space // 2
+    mine = s % 2 * size
+    send(
+        pieces.at[pl.ds(size - mine, size)], land, (send_1.at[0], recv_1.at[0]), (f, mate)
+    ).wait_recv()
+    pieces[pl.ds(mine, size)] = pieces[pl.ds(mine, size)] + land[...]
+
+    def chain(step, edge, end, arriving, leaving, i):
+        def copy(to):
+            return pltpu.make_async_remote_copy(
+                src_ref=leaving, dst_ref=arriving, send_sem=send_1.at[i], recv_sem=recv_1.at[i],
+                device_id=(f, to), device_id_type=MESH,
+            )
+
+        @pl.when(z == edge)
+        def _():
+            arriving[...] = jnp.zeros_like(arriving)
+
+        @pl.when(z != edge)
+        def _():
+            copy(s - step).wait_recv()
+
+        @pl.when(z != end)
+        def _():
+            leaving[...] = arriving[...] + pieces[pl.ds(mine, size)]
+            copy(s + step).start()
+
+    def go_up():
+        chain(2, 0, top, below, upward, 1)
+
+    def go_down():
+        chain(-2, top, 0, above, downward, 2)
+
+    @pl.when(2 * z <= top)
+    def _():
+        go_up()
+        go_down()
+
+    @pl.when(2 * z > top)
+    def _():
+        go_down()
+        go_up()
+
+    own[...] = ((below[...] + pieces[pl.ds(mine, size)] + above[...]) * factor).astype(own.dtype)
     second = []
     for df in range(1, n_freq):
         second.append(
-            send(own, every.at[base, f], (send_2.at[df], recv_2.at[df]), (lax.rem(f + df, n_freq), s))
-        )
-    for j, c in order[ahead:]:
+            send(
+                own, every.at[pl.ds(mine, size), f], (send_2.at[df], recv_2.at[df]), (lax.rem(f + df, n_freq), s)
+            )
+        )
+    for swap in order[ahead:]:
         for df in range(1, n_freq):
-            swap(j, c, df).start()
-    every[base, f] = own[...]
+            swap(df).start()
+    every[pl.ds(mine, size), f] = own[...]
     for copy in second:
         copy.wait_recv()
-    for i, mate in reversed(list(enumerate(mates))):
-        low, size = bases[i]
-        block = every.at[pl.ds(low, size)]
-        send(block, block, (send_3.at[i], recv_3.at[i]), (f, mate)).wait_recv()
+    block = every.at[pl.ds(mine, size)]
+    send(block, block, (send_3.at[0], recv_3.at[0]), (f, mate)).wait_recv()
 
     coefs = []
     for c in range(2):
@@ -277,14 +338,6 @@
 
     lax.fori_loop(0, groups, fill, 0)
 
-    def arrived(j):
-        for c in range(2):
-            keep(j, c).wait()
-            for df in range(1, n_freq):
-                swap(j, c, df).wait_recv()
-        for c in range(2):
-            taken[j, c, length] = taken[j, c, length // 2]
-
     half_length = length // 2
 
     def put_at(column, wide):
@@ -294,36 +347,61 @@
         return put
 
     def finish(j, carry):
-        tiles = (2 * j, 2 * j + 1)
-        for one in tiles:
-            arrived(one)
+        for c in range(2):
+            keep_broad(j, c).wait()
+            for r in range(2):
+                for df in range(1, n_freq):
+                    swap_broad(j, c, r, df).wait_recv()
+            broad[j, c, length] = broad[j, c, length // 2]
         synthesize(
-            lambda g: stack_modes(taken, tiles, g, length), left_ref, basis_ref, mid_ref, 2 * tile,
+            lambda g: stack_modes(broad, j, g, length), left_ref, basis_ref, mid_ref, 2 * tile,
             put_at(pl.multiple_of(j * 2 * tile, 2 * tile), 2 * tile),
         )
         return carry
 
-    early = chunks - 1
-    if early >= 2:
-        lax.fori_loop(0, early // 2, finish, 0)
-    if early % 2:
-        arrived(early - 1)
+    def arrived(j):
+        for c in range(2):
+            keep_narrow(j, c).wait()
+            for df in range(1, n_freq):
+                swap_narrow(j, c, df).wait_recv()
+            narrow[j, c, length] = narrow[j, c, length // 2]
+
+    if wides:
+        lax.fori_loop(0, wides, finish, 0)
+    last = narrows - 1
+    for j in range(last):
+        arrived(j)
         synthesize(
-            lambda g: stack_modes(taken, (early - 1,), g, length), left_ref, basis_ref, mid_ref, tile,
-            put_at((early - 1) * tile, tile),
-        )
-    arrived(early)
+            lambda g: stack_modes(narrow, j, g, length), left_ref, basis_ref, mid_ref, tile,
+            put_at((2 * wides + j) * tile, tile),
+        )
+    arrived(last)
 
     def arrange(g, carry):
-        late_ref[g] = stack_modes(taken, (early,), g, length)
+        late_ref[g] = stack_modes(narrow, last, g, length)
         return carry
 
     lax.fori_loop(0, groups, arrange, 0)
+
+    @pl.when(z < top)
+    def _():
+        pltpu.make_async_remote_copy(
+            src_ref=upward, dst_ref=below, send_sem=send_1.at[1], recv_sem=recv_1.at[1],
+            device_id=(f, s + 2), device_id_type=MESH,
+        ).wait_send()
+
+    @pl.when(z > 0)
+    def _():
+        pltpu.make_async_remote_copy(
+            src_ref=downward, dst_ref=above, send_sem=send_1.at[2], recv_sem=recv_1.at[2],
+            device_id=(f, s - 2), device_id_type=MESH,
+        ).wait_send()
+
     for copy in started:
         copy.wait_send()
-    for j, c in order:
+    for swap in order:
         for df in range(1, n_freq):
-            swap(j, c, df).wait_send()
+            swap(df).wait_send()
 
 
 def gather(spectra, eigvecs, weights, basis, n_freq, n_space, blocks, factor, tile):
@@ -333,7 +411,7 @@
     half = group * modes
     halves = count // group
     width = points // n_freq
-    chunks = width // tile
+    wides, narrows = width // (2 * tile) - 1, 2
     parts = 4
     cut = points // parts
     groups = length // (2 * PAIR)
@@ -349,36 +427,44 @@
     ]
     dma = pltpu.SemaphoreType.DMA
     return pl.pallas_call(
-        functools.partial(gather_kernel, n_freq, n_space, group, parts, factor),
+        functools.partial(gather_kernel, n_freq, n_space, group, parts, factor, wides),
         out_shape=out_shape,
         in_specs=[hbm] * 4,
         out_specs=[vmem] * len(out_shape),
         scratch_shapes=[
-            pltpu.VMEM((chunks, 2, length + 1, modes, tile), jnp.bfloat16),
+            pltpu.VMEM((max(wides, 1), 2, length + 1, modes, 2 * tile), jnp.bfloat16),
+            pltpu.VMEM((narrows, 2, length + 1, modes, tile), jnp.bfloat16),
             pltpu.VMEM((2, 2, group * blocks, cut), jnp.bfloat16),
             pltpu.VMEM((2, 2, group, modes, cut), jnp.bfloat16),
             pltpu.VMEM((points,), jnp.bfloat16),
             pltpu.VMEM((parts, 1, cut), jnp.float32),
             pltpu.VMEM((2 * halves, blocks, 2 * half), jnp.float32),
             pltpu.VMEM((n_space, rows, half), jnp.float32),
-            pltpu.VMEM((n_space, rows, half), jnp.float32),
-            pltpu.VMEM((rows, half), jnp.bfloat16),
+            pltpu.VMEM((n_space // 2, rows, half), jnp.float32),
+            pltpu.VMEM((n_space // 2, rows, half), jnp.float32),
+            pltpu.VMEM((n_space // 2, rows, half), jnp.float32),
+            pltpu.VMEM((n_space // 2, rows, half), jnp.float32),
+            pltpu.VMEM((n_space // 2, rows, half), jnp.float32),
+            pltpu.VMEM((n_space // 2, rows, half), jnp.bfloat16),
             pltpu.VMEM((n_space, n_freq, rows, half), jnp.bfloat16),
             pltpu.VMEM((groups, 2, blocks, depth), jnp.float32),
             pltpu.VMEM((blocks, length, 2 * tile), jnp.bfloat16),
             pltpu.VMEM((length, length), jnp.bfloat16),
-            dma((chunks, 2, n_freq)),
-            dma((chunks, 2, n_freq)),
-            dma((chunks, 2)),
+            dma((max(wides, 1), 2, 2, n_freq)),
+            dma((max(wides, 1), 2, 2, n_freq)),
+            dma((narrows, 2, n_freq)),
+            dma((narrows, 2, n_freq)),
+            dma((max(wides, 1), 2)),
+            dma((narrows, 2)),
             dma((2,)),
             dma((2,)),
             dma((2,)),
-            dma((n_space,)),
-            dma((n_space,)),
+            dma((3,)),
+            dma((3,)),
             dma((n_freq,)),
             dma((n_freq,)),
-            dma((n_space,)),
-            dma((n_space,)),
+            dma((1,)),
+            dma((1,)),
         ],
         compiler_params=pltpu.CompilerParams(
             collective_id=0, has_side_effects=True, vmem_limit_bytes=32 << 20

time: 58.6 us -> 57.9 us (0.988)
  Pallas kernels: 58.5 us -> 57.7 us
    pallas_call x1, Pallas kernels: 53.5 us -> 52.7 us  [gather(): pl.pallas_call(functools.partial(gather_kernel, n_freq, n_space, group, p...]
where the time goes in v2:
time: 57.9 us; the launch traced here: 57.7 us
  Pallas kernels  57.7 us (100%)
    pallas_call x1, Pallas kernels, gather(): pl.pallas_call(functools.partial(gather_kernel, n_freq, n_space, group, p...  52.7 us
    pallas_call x1, Pallas kernels, finish(): pl.pallas_call(finish_kernel, out_shape=jax.ShapeDtypeStruct((out_rows, w...  4.95 us

profile of v2, /device:TPU:0, one launch (start us, length us, event | category | flops | bytes accessed | tf_op | source)
XLA Modules:
  0.0 57.7 jit_solution(12415470456555026642)
XLA Ops:
  0.0 0.0 copy-start
  0.0 52.7 %gather.1 = (f32[3200,896]{1,0:T(8,128)S(1)}, bf16[8,256,128]{2,1,0:T(8,128)(2,1)S(1)}, bf16[8,768,256]{2,1,0:T(8,128)(2,1)S(1)}) custom-call(bf16[2,1536,4096]{2,1,0:T(8,128)(2,1)} %bitcast.1, bf16[2,64,4,4096]{3,2,1,0:T(4,128)(2,1)} %eigvecs_ref.1, bf16[4096]{0:T(1024)(128)(2,1)} %weights_ref.1, bf16[256,256]{1,0:T(8,128)(2,1)} %constant.3.basis_hbm.basis_ref), custom_call_target="tpu_custom_call" | custom-call | flops 12884901888 | bytes 50331648 | tf_op jit(solution)/shard_map/gather/pallas_call | solution.py:429
  52.8 0.0 copy-done
  52.8 5.0 %finish.1 = f32[3200,1024]{1,0:T(8,128)} custom-call(f32[3200,896]{1,0:T(8,128)S(1)} %get-tuple-element.8.early_ref, bf16[8,256,128]{2,1,0:T(8,128)(2,1)S(1)} %get-tuple-element.9.late_ref, bf16[8,768,256]{2,1,0:T(8,128)(2,1)S(1)} %get-tuple-element.10.left_ref, bf16[256,256]{1,0:T(8,128)(2,1)S(1)} %copy-done), custom_call_target="tpu_custom_call" | custom-call | flops 805306368 | bytes 13107200 | tf_op jit(solution)/shard_map/finish/pallas_call | solution.py:507
Async XLA Ops:
  0.0 52.8 %copy-start = (bf16[256,256]{1,0:T(8,128)(2,1)S(1)}, bf16[256,256]{1,0:T(8,128)(2,1)}, u32[]{:S(2)}) copy-start(bf16[256,256]{1,0:T(8,128)(2,1)} %constant.3.basis_hbm.basis_ref) | copy-start | bytes 393220
